TPU v7x, 32 devices: a whole 2x2x4 slice. The times are simulated.
32 devices in a mesh: seq: 8 (over z, y), head: 4 (over x, core).
Axes of the slice: x: 2, y: 2, z: 4, core: 2. Of those that a mesh axis runs over, the one named last changes fastest.
Arguments:
- queries: bfloat16 [4096, 2048], P('seq', 'head'), may hold values from -6 to 6
- key_vectors: bfloat16 [4096, 2048], P('seq', 'head'), may hold values from -6 to 6
- value_vectors: bfloat16 [4096, 2048], P('seq', 'head'), may hold values from -6 to 6
- gate_input: bfloat16 [4096, 2048], P('seq', 'head'), may hold values from -6 to 6
- out_weight: bfloat16 [2048, 4096], P('seq', 'head'), may hold values from -0.125 to 0.125
Outputs:
- layer_output: bfloat16 [4096, 4096], P('seq', 'head')
All inputs are finite; a program needn't handle non-finite values.
Results may differ from a plain program's by a relative error of at most 0.0057.
Values may be sent and summed in bfloat16 or wider, within the bound.
A program may use at most 64 MiB of HBM per device.

v0:
```python
import jax
import jax.numpy as jnp
from jax import lax
from jax.sharding import PartitionSpec as P

HD = 128


def carried_in(shard, axis, combine, identity):
    count, position = (lax.axis_size(axis), lax.axis_index(axis))
    everything = lax.all_gather(shard, axis)
    start = jnp.broadcast_to(jnp.asarray(identity, shard.dtype), shard.shape)

    def turn(k, before):
        reached = k < position
        new = combine(before, everything[k])
        return jnp.where(reached, new, before)

    return lax.fori_loop(0, count, turn, start)


def add_states(earlier, later):
    return earlier + later


def carried(own_state):
    return carried_in(own_state, "seq", add_states, jnp.zeros_like(own_state))


def in_shard(qhead, khead, vhead, scale):
    rows = qhead.shape[0]
    step = min(rows, 512)
    scores = jnp.einsum("thd,shd->hts", qhead, khead, preferred_element_type=jnp.float32) * scale
    rowpos = 0 + lax.broadcasted_iota(jnp.int32, (step, step), 0)
    colpos = lax.broadcasted_iota(jnp.int32, (step, step), 1)
    scores = jnp.where((colpos <= rowpos)[None, :, :], scores, 0.0).astype(jnp.bfloat16)
    pieces = jnp.einsum("hts,she->the", scores, vhead, preferred_element_type=jnp.float32)
    return pieces


def per_device(queries, key_vectors, value_vectors, gate_input, out_weight):
    rows, width = queries.shape
    heads = width // HD
    scale = HD ** (-0.5)
    qhead = queries.reshape(rows, heads, HD)
    khead = key_vectors.reshape(rows, heads, HD)
    vhead = value_vectors.reshape(rows, heads, HD)
    own_state = jnp.einsum("thd,the->hde", khead, vhead, preferred_element_type=jnp.float32)
    local = in_shard(qhead, khead, vhead, scale)
    prefix = carried(own_state)
    inter = (
        jnp.einsum(
            "thd,hde->the", qhead, prefix.astype(jnp.bfloat16), preferred_element_type=jnp.float32
        )
        * scale
    )
    attn = (local + inter).reshape(rows, width)
    squares = jnp.sum(attn * attn, axis=1)
    hidden = (attn * jax.nn.silu(gate_input.astype(jnp.float32))).astype(jnp.bfloat16)
    total = lax.psum(squares, "head")
    features = lax.all_gather(hidden, "head", axis=1, tiled=True)
    full_block = lax.all_gather(out_weight, "seq", axis=0, tiled=True)
    projected = jnp.dot(features, full_block, preferred_element_type=jnp.float32)
    mean_square = total / features.shape[1]
    return (projected * lax.rsqrt(mean_square + 1e-06)[:, None]).astype(jnp.bfloat16)


def solution(mesh):
    placed = (
        P("seq", "head"),
        P("seq", "head"),
        P("seq", "head"),
        P("seq", "head"),
        P("seq", "head"),
    )
    return jax.shard_map(
        per_device, mesh=mesh, in_specs=placed, out_specs=P("seq", "head"), check_vma=False
    )
```

profile of v0, /device:TPU:0, one launch (start us, length us, event | category | flops | bytes accessed | tf_op | source)
XLA Modules:
  0.0 184.2 jit_solution(1914398323355310470)
XLA Ops:
  6.5 0.0 copy-start
  6.5 0.0 all-gather.9.cloned.1.call-start
  6.5 1.3 copy.19
  7.9 2.0 %fusion.10 = f32[4,128,128]{2,1,0:T(8,128)} fusion(bf16[512,4,128]{0,2,1:T(8,128)(2,1)S(1)} %bitcast.47, bf16[512,512]{1,0:T(8,128)(2,1)} %param.9), kind=kOutput, calls=%fused_computation.18 | convolution fusion | flops 67108864 | bytes 1310720 | tf_op jit(solution)/shard_map/thd,the->hde/dot_general | solution.py:48
  9.9 0.0 all-gather.9.cloned.1.call-update
  9.9 0.0 all-gather.5.cloned.1.call-start
  10.0 0.1 iota_compare_fusion
  10.1 51.8 %all-gather.9.cloned.1.call-done = f32[32,128,128]{2,1,0:T(8,128)} async-done(((f32[4,128,128]{2,1,0:T(8,128)}), f32[32,128,128]{2,1,0:T(8,128)}) %all-gather.9.cloned.1.call-update) | async-done | bytes 2097168 | tf_op jit(solution)/shard_map/all_gather | solution.py:11
  61.9 8.5 %while.14 = (s32[]{:T(128)}, f32[4,128,128]{2,1,0:T(8,128)S(1)}, s32[]{:T(128)}, f32[8,4,128,128]{3,2,1,0:T(8,128)}, s32[]{:T(128)}, /*index=5*/s32[]{:T(128)}) while((s32[]{:T(128)}, f32[4,128,128]{2,1,0:T(8,128)S(1)}, s32[]{:T(128)}, f32[8,4,128,128]{3,2,1,0:T(8,128)}, s32[]{:T(128)}, /*index=5*/s32[]{:T(128)}) %tuple.42), condition=%wide.region_1.2_spmd.clone, body=%wide.region_0.1_spmd.clone.sunk | while | flops 196612 | bytes 786525 | solution.py:19
  61.9 1.0 add_select_fusion.2
  62.9 1.0 add_select_fusion.2
  64.0 1.0 add_select_fusion.2
  65.1 1.0 add_select_fusion.2
  66.1 1.0 add_select_fusion.2
  67.2 1.0 add_select_fusion.2
  68.3 1.0 add_select_fusion.2
  69.3 1.0 add_select_fusion.2
  70.4 0.0 copy-done
  70.4 0.3 fusion.3
  70.7 2.4 %multiply_reduce_fusion = (f32[512]{0:T(512)S(1)}, f32[512,4,128]{0,2,1:T(8,128)S(1)}) fusion(f32[512,4,128]{0,2,1:T(8,128)S(1)} %fusion.3, bf16[512,4,128]{0,2,1:T(8,128)(2,1)S(1)} %bitcast.48, pred[512,512]{1,0:T(8,128)(4,1)S(1)} %iota_compare_fusion, bf16[512,512]{1,0:T(8,128)(2,1)} %param.9, bf16[512,512]{1,0:T(8,128)(2,1)S(1)} %copy-done), kind=kOutput, calls=%fused_computation.14 | convolution fusion | flops 540802560 | bytes 3934208 | tf_op jit(solution)/shard_map/hts,she->the/dot_general | solution.py:37
  73.2 0.0 copy-start.1
  73.2 0.3 copy.17
  73.5 0.7 copy-done.1
  74.2 1.1 fusion.8
  75.3 0.0 all-gather.5.cloned.1.call-update
  75.3 0.0 all-gather.7.cloned.1.call-start
  75.4 0.7 all-gather.7.cloned.1.call-update
  76.1 5.7 %psum.7 = f32[512]{0:T(512)S(1)} all-reduce(f32[512]{0:T(512)S(1)} %get-tuple-element.108), channel_id=1, replica_groups=mesh['seq'=8,'head'=4] {'head'}, use_global_device_ids=true, to_apply=%region_3.4 | all-reduce | flops 512 | bytes 4096 | tf_op jit(solution)/shard_map/psum | solution.py:60
  81.8 14.8 %all-gather.5.cloned.1.call-done = bf16[512,2048]{1,0:T(8,128)(2,1)} async-done(((bf16[512,512]{1,0:T(8,128)(2,1)}), bf16[512,2048]{1,0:T(8,128)(2,1)}) %all-gather.5.cloned.1.call-update) | async-done | bytes 2097168 | tf_op jit(solution)/shard_map/all_gather | solution.py:61
  96.6 75.0 %all-gather.7.cloned.1.call-done = bf16[2048,1024]{1,0:T(8,128)(2,1)} async-done(((bf16[256,1024]{1,0:T(8,128)(2,1)}), bf16[2048,1024]{1,0:T(8,128)(2,1)}) %all-gather.7.cloned.1.call-update) | async-done | bytes 4194320 | tf_op jit(solution)/shard_map/all_gather | solution.py:62
  171.6 6.1 %multiply_convert_fusion = bf16[512,1024]{1,0:T(8,128)(2,1)} fusion(bf16[512,2048]{1,0:T(8,128)(2,1)} %all-gather.5.cloned.1.call-done, bf16[2048,1024]{1,0:T(8,128)(2,1)} %all-gather.7.cloned.1.call-done, f32[512]{0:T(512)S(1)} %add_rsqrt_fusion), kind=kOutput, calls=%fused_computation.2 | convolution fusion | flops 2148532224 | bytes 7342080 | tf_op jit(solution)/shard_map/dot_general | solution.py:63
  (2 shorter events, 0.0 us)
Async XLA Ops:
  6.5 63.9 %copy-start = (bf16[512,512]{1,0:T(8,128)(2,1)S(1)}, bf16[512,512]{1,0:T(8,128)(2,1)}, u32[]{:S(2)}) copy-start(bf16[512,512]{1,0:T(8,128)(2,1)} %param.7) | copy-start | bytes 1572868
  6.5 55.3 %all-gather.9.cloned.1.call-start = ((), (), s32[]{:S(2)}) async-start(), calls=%async_computation.2 | async-start | bytes 2359296 | tf_op jit(solution)/shard_map/all_gather | solution.py:11
  9.9 86.7 %all-gather.5.cloned.1.call-start = ((), (), s32[]{:S(2)}) async-start(), calls=%async_computation | async-start | bytes 2621440 | tf_op jit(solution)/shard_map/all_gather | solution.py:61
  73.2 1.0 copy-start.1
  75.3 96.2 %all-gather.7.cloned.1.call-start = ((), (), s32[]{:S(2)}) async-start(), calls=%async_computation.1 | async-start | bytes 4718592 | tf_op jit(solution)/shard_map/all_gather | solution.py:62
Sparse Core Ops, SparseCore 0:
  10.0 51.7 all-gather.8
  75.5 21.0 all-gather.4
  98.7 72.7 all-gather.6
where the time goes:
time: 185 us; the launch traced here: 184 us
  waiting for transfers between devices  142 us (77%)
  between operations  13.2 us (7%)
  matrix products  10.9 us (6%)
  other arithmetic  9.53 us (5%)
  blocking collectives  5.67 us (3%)
  local copies, waits for them, and re-layouts  2.34 us (1%)
    all_gather x1, waiting for transfers between devices, per_device(): full_block = lax.all_gather(out_weight, 'seq', axis=0, tiled=True)  75 us
    all_gather x1, waiting for transfers between devices, carried_in(): everything = lax.all_gather(shard, axis)  51.8 us
    all_gather x1, waiting for transfers between devices, per_device(): features = lax.all_gather(hidden, 'head', axis=1, tiled=True)  14.8 us
    select_n x8, other arithmetic, turn(): return jnp.where(reached, new, before)  8.32 us
    dot_general x1, matrix products, per_device(): jnp.dot(features, full_block, preferred_element_type=jnp.float32)  6.12 us
    psum x1, blocking collectives, per_device(): total = lax.psum(squares, 'head')  5.67 us
  transfers between devices with their start and end apart: 3, of which 3 were waited for; matrix products, arithmetic and copies ran while one was open for 0% of the time, Pallas kernels for 0%

commit v1 on v0

--- a/solution.py
+++ b/solution.py
@@ -4,6 +4,16 @@
 from jax.sharding import PartitionSpec as P
 
 HD = 128
+
+
+def turned_line(x, name, dim):
+    size = lax.axis_size(name)
+    held, pieces = (x, [x])
+    for _ in range(size - 1):
+        held = lax.ppermute(held, name, [(i, (i + 1) % size) for i in range(size)])
+        pieces.insert(0, held)
+    flat = jnp.concatenate(pieces, axis=dim)
+    return jnp.roll(flat, (lax.axis_index(name) + 1) * x.shape[dim], axis=dim)
 
 
 def carried_in(shard, axis, combine, identity):
@@ -59,7 +69,7 @@
     hidden = (attn * jax.nn.silu(gate_input.astype(jnp.float32))).astype(jnp.bfloat16)
     total = lax.psum(squares, "head")
     features = lax.all_gather(hidden, "head", axis=1, tiled=True)
-    full_block = lax.all_gather(out_weight, "seq", axis=0, tiled=True)
+    full_block = turned_line(out_weight, "seq", 0)
     projected = jnp.dot(features, full_block, preferred_element_type=jnp.float32)
     mean_square = total / features.shape[1]
     return (projected * lax.rsqrt(mean_square + 1e-06)[:, None]).astype(jnp.bfloat16)

time: 185 us -> 163 us (0.88)
  waiting for transfers between devices: 142 us -> 98.3 us
  local copies, waits for them, and re-layouts: 2.34 us -> 15 us
  starting transfers between devices: 0.09 us -> 4.13 us
  matrix products: 10.9 us -> 13.2 us
  other arithmetic: 9.53 us -> 11.4 us
    ppermute x0 -> x7, waiting for transfers between devices: none -> 98.3 us  [turned_line(): held = lax.ppermute(held, name, [(i, (i + 1) % size) for i in range(size)])]
    all_gather x1 -> x0, waiting for transfers between devices: 75 us -> none  [per_device(): full_block = lax.all_gather(out_weight, 'seq', axis=0, tiled=True)]
    all_gather x1, waiting for transfers between devices: 51.8 us -> 0.01 us  [carried_in(): everything = lax.all_gather(shard, axis)]
    all_gather x1, waiting for transfers between devices: 14.8 us -> 0.01 us  [per_device(): features = lax.all_gather(hidden, 'head', axis=1, tiled=True)]
    unnamed x4 -> x31, local copies, waits for them, and re-layouts: 0.7 us -> 12.1 us
    ppermute x0 -> x7, starting transfers between devices: none -> 4.09 us  [turned_line(): held = lax.ppermute(held, name, [(i, (i + 1) % size) for i in range(size)])]
  transfers between devices with their start and end apart: 3 -> 9, of which waited for: 3 -> 6; matrix products, arithmetic and copies ran while one was open for 0% -> 17% of each run, Pallas kernels for 0% -> 0%
where the time goes in v1:
time: 163 us; the launch traced here: 162 us
  waiting for transfers between devices  98.3 us (60%)
  local copies, waits for them, and re-layouts  15 us (9%)
  between operations  13.6 us (8%)
  matrix products  13.2 us (8%)
  other arithmetic  11.4 us (7%)
  blocking collectives  6.39 us (4%)
  starting transfers between devices  4.13 us (3%)
    ppermute x7, waiting for transfers between devices, turned_line(): held = lax.ppermute(held, name, [(i, (i + 1) % size) for i in range(size)])  98.3 us
    unnamed x31, local copies, waits for them, and re-layouts  12.1 us
    select_n x8, other arithmetic, turn(): return jnp.where(reached, new, before)  8.32 us
    psum x1, blocking collectives, per_device(): total = lax.psum(squares, 'head')  6.39 us
    dot_general x1, matrix products, per_device(): jnp.dot(features, full_block, preferred_element_type=jnp.float32)  6.13 us
    ppermute x7, starting transfers between devices, turned_line(): held = lax.ppermute(held, name, [(i, (i + 1) % size) for i in range(size)])  4.09 us
    dot_general x1, matrix products, in_shard(): jnp.einsum('hts,she->the', scores, vhead, preferred_element_type=jnp.floa...  3.69 us
  transfers between devices with their start and end apart: 9, of which 6 were waited for; matrix products, arithmetic and copies ran while one was open for 17% of the time, Pallas kernels for 0%

profile of v1, /device:TPU:0, one launch (start us, length us, event | category | flops | bytes accessed | tf_op | source)
XLA Modules:
  0.0 162.2 jit_solution(7619510253483718318)
XLA Ops:
  6.5 0.0 copy-start
  6.5 0.0 all-gather.6.cloned.1.call-start
  6.5 1.3 copy.19
  7.9 2.0 %fusion.14 = f32[4,128,128]{2,1,0:T(8,128)} fusion(bf16[512,4,128]{0,2,1:T(8,128)(2,1)S(1)} %bitcast.46, bf16[512,512]{1,0:T(8,128)(2,1)} %param.9), kind=kOutput, calls=%fused_computation.20 | convolution fusion | flops 67108864 | bytes 1310720 | tf_op jit(solution)/shard_map/thd,the->hde/dot_general | solution.py:58
  9.9 0.0 all-gather.6.cloned.1.call-update
  10.0 0.0 all-gather.4.cloned.1.call-start
  10.0 3.0 %collective-permute-start = (bf16[256,1024]{1,0:T(8,128)(2,1)}, bf16[256,1024]{1,0:T(8,128)(2,1)S(1)}, u32[]{:S(2)}, u32[]{:S(2)}) collective-permute-start(bf16[256,1024]{1,0:T(8,128)(2,1)} %param.11), channel_id=1, source_target_pairs={{0,4},{4,8},{8,12},{12,16},{16,20},{20,24},{24,28},{28,0},{1,5},{5... | collective-permute-start | bytes 1572872 | tf_op jit(solution)/shard_map/ppermute | solution.py:13
  13.0 17.8 %collective-permute-done = bf16[256,1024]{1,0:T(8,128)(2,1)S(1)} collective-permute-done((bf16[256,1024]{1,0:T(8,128)(2,1)}, bf16[256,1024]{1,0:T(8,128)(2,1)S(1)}, u32[]{:S(2)}, u32[]{:S(2)}) %collective-permute-start) | collective-permute-done | bytes 524320 | tf_op jit(solution)/shard_map/ppermute | solution.py:13
  30.9 0.0 collective-permute-start.1
  30.9 17.2 %collective-permute-done.1 = bf16[256,1024]{1,0:T(8,128)(2,1)S(1)} collective-permute-done((bf16[256,1024]{1,0:T(8,128)(2,1)S(1)}, bf16[256,1024]{1,0:T(8,128)(2,1)S(1)}, u32[]{:S(2)}, u32[]{:S(2)}) %collective-permute-start.1) | collective-permute-done | bytes 524320 | tf_op jit(solution)/shard_map/ppermute | solution.py:13
  48.1 0.0 collective-permute-start.2
  48.1 23.5 %collective-permute-done.2 = bf16[256,1024]{1,0:T(8,128)(2,1)S(1)} collective-permute-done((bf16[256,1024]{1,0:T(8,128)(2,1)S(1)}, bf16[256,1024]{1,0:T(8,128)(2,1)S(1)}, u32[]{:S(2)}, u32[]{:S(2)}) %collective-permute-start.2) | collective-permute-done | bytes 524320 | tf_op jit(solution)/shard_map/ppermute | solution.py:13
  71.6 1.0 collective-permute-start.3
  72.5 15.8 %collective-permute-done.3 = bf16[256,1024]{1,0:T(8,128)(2,1)S(1)} collective-permute-done((bf16[256,1024]{1,0:T(8,128)(2,1)S(1)}, bf16[256,1024]{1,0:T(8,128)(2,1)S(1)}, u32[]{:S(2)}, u32[]{:S(2)}) %collective-permute-start.3) | collective-permute-done | bytes 524320 | tf_op jit(solution)/shard_map/ppermute | solution.py:13
  88.3 0.0 collective-permute-start.4
  88.3 0.0 copy-done.2
  88.4 0.9 iota_compare_fusion
  89.2 15.1 %collective-permute-done.4 = bf16[256,1024]{1,0:T(8,128)(2,1)} collective-permute-done((bf16[256,1024]{1,0:T(8,128)(2,1)S(1)}, bf16[256,1024]{1,0:T(8,128)(2,1)}, u32[]{:S(2)}, u32[]{:S(2)}) %collective-permute-start.4) | collective-permute-done | bytes 524320 | tf_op jit(solution)/shard_map/ppermute | solution.py:13
  104.3 0.0 collective-permute-start.5
  104.3 8.5 %while.14 = (s32[]{:T(128)}, f32[4,128,128]{2,1,0:T(8,128)S(1)}, s32[]{:T(128)}, f32[8,4,128,128]{3,2,1,0:T(8,128)}, s32[]{:T(128)}, /*index=5*/s32[]{:T(128)}) while((s32[]{:T(128)}, f32[4,128,128]{2,1,0:T(8,128)S(1)}, s32[]{:T(128)}, f32[8,4,128,128]{3,2,1,0:T(8,128)}, s32[]{:T(128)}, /*index=5*/s32[]{:T(128)}) %tuple.40), condition=%wide.region_1.2_spmd.clone, body=%wide.region_0.1_spmd.clone.sunk | while | flops 196612 | bytes 786525 | solution.py:29
  104.3 1.0 add_select_fusion.2
  105.4 1.0 add_select_fusion.2
  106.5 1.0 add_select_fusion.2
  107.5 1.0 add_select_fusion.2
  108.6 1.0 add_select_fusion.2
  109.6 1.0 add_select_fusion.2
  110.7 1.0 add_select_fusion.2
  111.8 1.0 add_select_fusion.2
  112.8 1.3 fusion.7
  114.2 3.7 %multiply_reduce_fusion = (f32[512]{0:T(512)S(1)}, f32[512,4,128]{0,2,1:T(8,128)}) fusion(f32[512,4,128]{0,2,1:T(8,128)} %fusion.7, bf16[512,4,128]{0,2,1:T(8,128)(2,1)S(1)} %bitcast.47, pred[512,512]{1,0:T(8,128)(4,1)} %iota_compare_fusion, bf16[512,512]{1,0:T(8,128)(2,1)S(1)} %copy-done.6, bf16[512,512]{1,0:T(8,128)(2,1)S(1)} %copy-done), kind=kOutput, calls=%fused_computation.16 | convolution fusion | flops 540802560 | bytes 3934208 | tf_op jit(solution)/shard_map/hts,she->the/dot_general | solution.py:47
  117.9 1.6 copy.17
  119.4 2.2 %fusion.12 = bf16[512,512]{1,0:T(8,128)(2,1)} fusion(f32[512,512]{1,0:T(8,128)S(1)} %copy.17, bf16[512,512]{1,0:T(8,128)(2,1)} %param.10), kind=kLoop, calls=%fused_computation.18 | loop fusion | flops 1835008 | bytes 2097152 | tf_op jit(solution)/shard_map/convert_element_type | solution.py:69
  121.6 0.0 all-gather.4.cloned.1.call-update
  121.6 0.0 collective-permute-done.5
  121.6 0.1 collective-permute-start.6
  121.7 6.4 %psum.7 = f32[512]{0:T(512)S(1)} all-reduce(f32[512]{0:T(512)S(1)} %get-tuple-element.108), channel_id=1, replica_groups=mesh['seq'=8,'head'=4] {'head'}, use_global_device_ids=true, to_apply=%region_3.4 | all-reduce | flops 512 | bytes 4096 | tf_op jit(solution)/shard_map/psum | solution.py:70
  128.1 8.9 %collective-permute-done.6 = bf16[256,1024]{1,0:T(8,128)(2,1)} collective-permute-done((bf16[256,1024]{1,0:T(8,128)(2,1)}, bf16[256,1024]{1,0:T(8,128)(2,1)}, u32[]{:S(2)}, u32[]{:S(2)}) %collective-permute-start.6) | collective-permute-done | bytes 524320 | tf_op jit(solution)/shard_map/ppermute | solution.py:13
  137.0 1.1 constant_dynamic-update-slice_fusion.15
  138.1 1.1 constant_dynamic-update-slice_fusion.14
  139.2 1.1 constant_dynamic-update-slice_fusion.13
  140.2 1.1 constant_dynamic-update-slice_fusion.12
  141.3 1.1 constant_dynamic-update-slice_fusion.11
  142.5 1.1 constant_dynamic-update-slice_fusion.7
  143.6 1.1 constant_dynamic-update-slice_fusion.6
  144.7 1.1 constant_dynamic-update-slice_fusion.5
  146.0 0.0 copy-start.7
  146.0 3.2 %copy-done.7 = bf16[4096,1024]{1,0:T(8,128)(2,1)} copy-done((bf16[4096,1024]{1,0:T(8,128)(2,1)}, bf16[4096,1024]{1,0:T(8,128)(2,1)S(1)}, u32[]{:S(2)}) %copy-start.7) | copy-done | bytes 8388632
  149.3 6.1 %multiply_convert_fusion = bf16[512,1024]{1,0:T(8,128)(2,1)} fusion(bf16[512,2048]{1,0:T(8,128)(2,1)} %all-gather.4.cloned.1.call-done, bf16[4096,1024]{1,0:T(8,128)(2,1)} %copy-done.7, s32[]{:T(128)S(6)} %select_n.40, f32[512]{0:T(512)S(1)} %add_rsqrt_fusion), kind=kOutput, calls=%fused_computation.4 | convolution fusion | flops 2148532224 | bytes 7342084 | tf_op jit(solution)/shard_map/dot_general | solution.py:73
  (24 shorter events, 0.3 us)
Async XLA Ops:
  6.5 106.3 %copy-start = (bf16[512,512]{1,0:T(8,128)(2,1)S(1)}, bf16[512,512]{1,0:T(8,128)(2,1)}, u32[]{:S(2)}) copy-start(bf16[512,512]{1,0:T(8,128)(2,1)} %param.7) | copy-start | bytes 1572868
  6.5 107.6 %copy-start.6 = (bf16[512,512]{1,0:T(8,128)(2,1)S(1)}, bf16[512,512]{1,0:T(8,128)(2,1)}, u32[]{:S(2)}) copy-start(bf16[512,512]{1,0:T(8,128)(2,1)} %param.9) | copy-start | bytes 1572868
  6.5 97.8 %all-gather.6.cloned.1.call-start = ((), (), s32[]{:S(2)}) async-start(), calls=%async_computation.1 | async-start | bytes 2359296 | tf_op jit(solution)/shard_map/all_gather | solution.py:21
  10.0 139.3 %all-gather.4.cloned.1.call-start = ((), (), s32[]{:S(2)}) async-start(), calls=%async_computation | async-start | bytes 2621440 | tf_op jit(solution)/shard_map/all_gather | solution.py:71
  10.0 20.9 %collective-permute-start = (bf16[256,1024]{1,0:T(8,128)(2,1)}, bf16[256,1024]{1,0:T(8,128)(2,1)S(1)}, u32[]{:S(2)}, u32[]{:S(2)}) collective-permute-start(bf16[256,1024]{1,0:T(8,128)(2,1)} %param.11), channel_id=1, source_target_pairs={{0,4},{4,8},{8,12},{12,16},{16,20},{20,24},{24,28},{28,0},{1,5},{5... | collective-permute-start | bytes 1572872 | tf_op jit(solution)/shard_map/ppermute | solution.py:13
  30.9 17.2 %collective-permute-start.1 = (bf16[256,1024]{1,0:T(8,128)(2,1)S(1)}, bf16[256,1024]{1,0:T(8,128)(2,1)S(1)}, u32[]{:S(2)}, u32[]{:S(2)}) collective-permute-start(bf16[256,1024]{1,0:T(8,128)(2,1)S(1)} %collective-permute-done), channel_id=1, source_target_pairs={{0,4},{4,8},{8,12},{12,16},{16,20},{20,24},{24,28},{28,0},{1,5},{5... | collective-permute-start | bytes 1572872 | tf_op jit(solution)/shard_map/ppermute | solution.py:13
  48.1 23.5 %collective-permute-start.2 = (bf16[256,1024]{1,0:T(8,128)(2,1)S(1)}, bf16[256,1024]{1,0:T(8,128)(2,1)S(1)}, u32[]{:S(2)}, u32[]{:S(2)}) collective-permute-start(bf16[256,1024]{1,0:T(8,128)(2,1)S(1)} %collective-permute-done.1), channel_id=1, source_target_pairs={{0,4},{4,8},{8,12},{12,16},{16,20},{20,24},{24,28},{28,0},{1,5},{5... | collective-permute-start | bytes 1572872 | tf_op jit(solution)/shard_map/ppermute | solution.py:13
  71.6 16.8 %copy-start.2 = (bf16[256,1024]{1,0:T(8,128)(2,1)}, bf16[256,1024]{1,0:T(8,128)(2,1)S(1)}, u32[]{:S(2)}) copy-start(bf16[256,1024]{1,0:T(8,128)(2,1)S(1)} %collective-permute-done.2) | copy-start | bytes 1572868
  71.6 16.8 %collective-permute-start.3 = (bf16[256,1024]{1,0:T(8,128)(2,1)S(1)}, bf16[256,1024]{1,0:T(8,128)(2,1)S(1)}, u32[]{:S(2)}, u32[]{:S(2)}) collective-permute-start(bf16[256,1024]{1,0:T(8,128)(2,1)S(1)} %collective-permute-done.2), channel_id=1, source_target_pairs={{0,4},{4,8},{8,12},{12,16},{16,20},{20,24},{24,28},{28,0},{1,5},{5... | collective-permute-start | bytes 1572872 | tf_op jit(solution)/shard_map/ppermute | solution.py:13
  88.3 24.5 %copy-start.4 = (bf16[256,1024]{1,0:T(8,128)(2,1)}, bf16[256,1024]{1,0:T(8,128)(2,1)S(1)}, u32[]{:S(2)}) copy-start(bf16[256,1024]{1,0:T(8,128)(2,1)S(1)} %collective-permute-done.3) | copy-start | bytes 1572868
  88.3 16.0 %collective-permute-start.4 = (bf16[256,1024]{1,0:T(8,128)(2,1)S(1)}, bf16[256,1024]{1,0:T(8,128)(2,1)}, u32[]{:S(2)}, u32[]{:S(2)}) collective-permute-start(bf16[256,1024]{1,0:T(8,128)(2,1)S(1)} %collective-permute-done.3), channel_id=1, source_target_pairs={{0,4},{4,8},{8,12},{12,16},{16,20},{20,24},{24,28},{28,0},{1,5},{5... | collective-permute-start | bytes 1572872 | tf_op jit(solution)/shard_map/ppermute | solution.py:13
  104.3 17.3 %collective-permute-start.5 = (bf16[256,1024]{1,0:T(8,128)(2,1)}, bf16[256,1024]{1,0:T(8,128)(2,1)}, u32[]{:S(2)}, u32[]{:S(2)}) collective-permute-start(bf16[256,1024]{1,0:T(8,128)(2,1)} %collective-permute-done.4), channel_id=1, source_target_pairs={{0,4},{4,8},{8,12},{12,16},{16,20},{20,24},{24,28},{28,0},{1,5},{5... | collective-permute-start | bytes 1572872 | tf_op jit(solution)/shard_map/ppermute | solution.py:13
  114.2 28.3 %copy-start.1 = (bf16[256,1024]{1,0:T(8,128)(2,1)S(1)}, bf16[256,1024]{1,0:T(8,128)(2,1)}, u32[]{:S(2)}) copy-start(bf16[256,1024]{1,0:T(8,128)(2,1)} %param.11) | copy-start | bytes 1572868
  121.6 24.2 %copy-start.5 = (bf16[256,1024]{1,0:T(8,128)(2,1)S(1)}, bf16[256,1024]{1,0:T(8,128)(2,1)}, u32[]{:S(2)}) copy-start(bf16[256,1024]{1,0:T(8,128)(2,1)} %copy-done.4) | copy-start | bytes 1572868
  121.6 24.3 %copy-start.3 = (bf16[256,1024]{1,0:T(8,128)(2,1)S(1)}, bf16[256,1024]{1,0:T(8,128)(2,1)}, u32[]{:S(2)}) copy-start(bf16[256,1024]{1,0:T(8,128)(2,1)} %copy-done.2) | copy-start | bytes 1572868
  121.6 15.4 %collective-permute-start.6 = (bf16[256,1024]{1,0:T(8,128)(2,1)}, bf16[256,1024]{1,0:T(8,128)(2,1)}, u32[]{:S(2)}, u32[]{:S(2)}) collective-permute-start(bf16[256,1024]{1,0:T(8,128)(2,1)} %collective-permute-done.5), channel_id=1, source_target_pairs={{0,4},{4,8},{8,12},{12,16},{16,20},{20,24},{24,28},{28,0},{1,5},{5... | collective-permute-start | bytes 1572872 | tf_op jit(solution)/shard_map/ppermute | solution.py:13
  146.0 3.2 %copy-start.7 = (bf16[4096,1024]{1,0:T(8,128)(2,1)}, bf16[4096,1024]{1,0:T(8,128)(2,1)S(1)}, u32[]{:S(2)}) copy-start(bf16[4096,1024]{1,0:T(8,128)(2,1)S(1)} %constant_dynamic-update-slice_fusion) | copy-start | bytes 25165828
Sparse Core Ops, SparseCore 0:
  10.1 64.1 all-gather.5
  121.7 24.7 all-gather.3
